TPU v7x, 128 devices: a whole 4x4x4 slice. The times are simulated.
128 devices in a mesh: dp: 1, sp: 16 (over z, y), tp: 8 (over x, core).
Axes of the slice: x: 4, y: 4, z: 4, core: 2. Of those that a mesh axis runs over, the one named last changes fastest.
Arguments:
- hidden_in: bfloat16 [4096, 5120], P(('dp', 'sp', 'tp'))
- segment_ids: int32 [4096], P(('dp', 'sp', 'tp'))
- positions: int32 [4096], P(('dp', 'sp', 'tp'))
- attn_gain: bfloat16 [2, 5120], replicated
- w_q: bfloat16 [2, 5120, 4096], P(None, None, 'tp')
- w_k: bfloat16 [2, 5120, 1024], P(None, None, 'tp')
- w_v: bfloat16 [2, 5120, 1024], P(None, None, 'tp')
- w_o: bfloat16 [2, 4096, 5120], P(None, 'tp')
- mlp_gain: bfloat16 [2, 5120], replicated
- w_gate: bfloat16 [2, 5120, 14336], P(None, None, 'tp')
- w_up: bfloat16 [2, 5120, 14336], P(None, None, 'tp')
- w_down: bfloat16 [2, 14336, 5120], P(None, 'tp')
Outputs:
- output 1: bfloat16 [4096, 5120], P(('dp', 'sp', 'tp'))
- output 2: bfloat16 [2, 4096, 8, 128], P(None, ('dp', 'sp'), 'tp')
- output 3: bfloat16 [2, 4096, 8, 128], P(None, ('dp', 'sp'), 'tp')
All inputs are finite; a program needn't handle non-finite values.
Results may differ from a plain program's by a relative error of at most 0.0178663.
Values are sent between devices in bfloat16 or wider.
A program may use at most 1 GiB of HBM per device.

v0:
```python
import math
import jax
import jax.numpy as jnp
from jax import lax
from jax.sharding import PartitionSpec as P

HEAD_DIM = 128
ROPE_BASE = 1e4
NORM_EPS = 1e-5
SCORE_SCALE = HEAD_DIM ** -0.5


def rms_norm(hidden, gain_vec):
    hidden32 = hidden.astype(jnp.float32)
    inv_rms = lax.rsqrt(jnp.mean(hidden32 * hidden32, axis=-1, keepdims=True) + NORM_EPS)
    return (hidden32 * inv_rms * gain_vec.astype(jnp.float32)).astype(jnp.bfloat16)


def rotary(rot_in, positions):
    half_dim = HEAD_DIM // 2
    inv_freq = ROPE_BASE ** (-jnp.arange(half_dim, dtype=jnp.float32) / half_dim)
    angles = positions.astype(jnp.float32)[..., None] * inv_freq
    cos_val = jnp.cos(angles)[..., None, :]
    sin_val = jnp.sin(angles)[..., None, :]
    first_half = rot_in[..., :half_dim]
    second_half = rot_in[..., half_dim:]
    return jnp.concatenate([first_half * cos_val - second_half * sin_val, second_half * cos_val + first_half * sin_val], axis=-1)


def attention_rows(q_rot, k_keys, v_keys, row_index, row_seg, key_seg):
    n_rows, n_kv, group_size = q_rot.shape[0], q_rot.shape[1], q_rot.shape[2]
    blk_rows = math.gcd(n_rows, 128)
    n_blocks = n_rows // blk_rows
    key_index = jnp.arange(k_keys.shape[0])

    def one_block(block_in):
        q_blk, idx_blk, seg_blk = block_in
        scores = jnp.einsum('qkgd,skd->kgqs', q_blk, k_keys, preferred_element_type=jnp.float32) * SCORE_SCALE
        allowed = (idx_blk[:, None] >= key_index[None, :]) & (seg_blk[:, None] == key_seg[None, :])
        probs = jax.nn.softmax(jnp.where(allowed, scores, -1e30), axis=-1).astype(jnp.bfloat16)
        return jnp.einsum('kgqs,skd->kgqd', probs, v_keys, preferred_element_type=jnp.float32).astype(jnp.bfloat16)

    blocks = (q_rot.reshape(n_blocks, blk_rows, n_kv, group_size, HEAD_DIM),
              row_index.reshape(n_blocks, blk_rows), row_seg.reshape(n_blocks, blk_rows))
    return lax.map(one_block, blocks)


def solution(mesh):
    n_tp = mesh.shape['tp']
    tok_spec = P(('dp', 'sp', 'tp'))
    col_spec = P(None, None, 'tp')
    row_spec = P(None, 'tp', None)
    cache_spec = P(None, ('dp', 'sp'), 'tp', None)

    def device_fn(hidden_in, segment_ids, positions, attn_gain, w_q, w_k, w_v, w_o, mlp_gain, w_gate, w_up, w_down):
        tok_local, model_dim = hidden_in.shape
        n_rows = tok_local * n_tp
        n_kv = w_k.shape[2] // HEAD_DIM
        group_size = w_q.shape[2] // HEAD_DIM // n_kv
        row_seg = lax.all_gather(segment_ids, 'tp', tiled=True)
        row_pos = lax.all_gather(positions, 'tp', tiled=True)
        key_seg = lax.all_gather(row_seg, 'sp', tiled=True)
        row_index = lax.axis_index('sp') * n_rows + jnp.arange(n_rows)
        hidden = hidden_in
        k_list = []
        v_list = []
        for layer_idx in range(w_q.shape[0]):
            normed = lax.all_gather(rms_norm(hidden, attn_gain[layer_idx]), 'tp', axis=0, tiled=True)
            q_lin = jnp.dot(normed, w_q[layer_idx], preferred_element_type=jnp.float32).reshape(n_rows, n_kv * group_size, HEAD_DIM)
            k_lin = jnp.dot(normed, w_k[layer_idx], preferred_element_type=jnp.float32).reshape(n_rows, n_kv, HEAD_DIM)
            v_rows = jnp.dot(normed, w_v[layer_idx], preferred_element_type=jnp.float32).astype(jnp.bfloat16).reshape(n_rows, n_kv, HEAD_DIM)
            q_rot = rotary(q_lin, row_pos).astype(jnp.bfloat16).reshape(n_rows, n_kv, group_size, HEAD_DIM)
            k_rows = rotary(k_lin, row_pos).astype(jnp.bfloat16)
            k_keys = lax.all_gather(k_rows, 'sp', axis=0, tiled=True)
            v_keys = lax.all_gather(v_rows, 'sp', axis=0, tiled=True)
            att_out = attention_rows(q_rot, k_keys, v_keys, row_index, row_seg, key_seg)
            wo_heads = w_o[layer_idx].reshape(n_kv, group_size, HEAD_DIM, model_dim)
            part_sum = jnp.einsum('nkgqd,kgdm->nqm', att_out, wo_heads, preferred_element_type=jnp.float32).astype(jnp.bfloat16).reshape(n_rows, model_dim)
            attn_res = lax.psum_scatter(part_sum, 'tp', scatter_dimension=0, tiled=True)
            hidden_mid = (hidden.astype(jnp.float32) + attn_res.astype(jnp.float32)).astype(jnp.bfloat16)
            normed_mlp = lax.all_gather(rms_norm(hidden_mid, mlp_gain[layer_idx]), 'tp', axis=0, tiled=True)
            gate_lin = jnp.dot(normed_mlp, w_gate[layer_idx], preferred_element_type=jnp.float32)
            up_lin = jnp.dot(normed_mlp, w_up[layer_idx], preferred_element_type=jnp.float32)
            act_vals = (jax.nn.silu(gate_lin) * up_lin).astype(jnp.bfloat16)
            down_part = jnp.dot(act_vals, w_down[layer_idx], preferred_element_type=jnp.float32).astype(jnp.bfloat16)
            mlp_res = lax.psum_scatter(down_part, 'tp', scatter_dimension=0, tiled=True)
            hidden = (hidden_mid.astype(jnp.float32) + mlp_res.astype(jnp.float32)).astype(jnp.bfloat16)
            k_list.append(k_rows)
            v_list.append(v_rows)
        return hidden, jnp.stack(k_list), jnp.stack(v_list)

    return jax.shard_map(device_fn, mesh=mesh,
                         in_specs=(P(('dp', 'sp', 'tp'), None), tok_spec, tok_spec, P(), col_spec, col_spec, col_spec, row_spec, P(), col_spec, col_spec, row_spec),
                         out_specs=(P(('dp', 'sp', 'tp'), None), cache_spec, cache_spec), check_vma=False)
```

profile of v0, /device:TPU:1, one launch (start us, length us, event | category | flops | bytes accessed | tf_op | source)
XLA Modules:
  0.0 551.3 jit_solution(9149633949607086246)
XLA Ops:
  7.2 0.8 slice_convert_fusion.1
  8.1 1.1 fusion.122
  9.2 1.9 fusion.124
  11.1 1.2 dynamic-slice
  13.0 0.9 dynamic-update-slice
  13.9 0.8 dynamic-update-slice.1
  14.7 8.5 %all-reduce.2 = (s32[256]{0:T(256)S(1)}, s32[256]{0:T(256)S(1)}) all-reduce(s32[256]{0:T(256)S(1)} %dynamic-update-slice, s32[256]{0:T(256)S(1)} %dynamic-update-slice.1), channel_id=1, replica_groups=mesh['dp'=1,'sp'=16,'tp'=8] {'tp'}, use_global_device_ids=true, to_apply=%add | all-reduce | flops 512 | bytes 4096
  23.3 17.6 %all-gather.12.cloned.1.call-done = bf16[256,5120]{1,0:T(8,128)(2,1)} async-done(((bf16[32,5120]{1,0:T(8,128)(2,1)}), bf16[256,5120]{1,0:T(8,128)(2,1)}) %all-gather.12.cloned.1.call-update) | async-done | bytes 2621456 | tf_op jit(solution)/shard_map/all_gather | solution.py:68
  40.9 3.1 fusion.108
  44.3 0.6 copy-done.4
  44.9 0.6 pad_maximum_fusion.3
  45.6 8.7 %slice_bitcast_fusion.1 = (bf16[512,5120]{0,1:T(8,128)(2,1)}, bf16[512,5120]{0,1:T(8,128)(2,1)}) fusion(bf16[2,5120,512]{2,1,0:T(8,128)(2,1)} %param.20), kind=kLoop, calls=%fused_computation.67 | loop fusion | bytes 20971520 | tf_op jit(solution)/shard_map/dot_general | solution.py:69
  54.4 8.0 %copy.24 = bf16[512,5120]{1,0:T(8,128)(2,1)} copy(bf16[512,5120]{0,1:T(8,128)(2,1)} %get-tuple-element.217) | data formatting | bytes 10485760 | tf_op jit(solution)/shard_map/dot_general | solution.py:69
  62.4 18.9 %all-gather.2 = s32[16,1,256]{2,1,0:T(1,128)S(1)} all-gather(s32[1,1,256]{2,1,0:T(1,128)S(1)} %bitcast.251), channel_id=1, replica_groups=mesh['dp'=1,'sp'=16,'tp'=8] {'sp'}, dimensions={0}, use_global_device_ids=true | all-gather | bytes 17408 | tf_op jit(solution)/shard_map/all_gather | solution.py:62
  81.6 2.8 fusion.114
  84.6 8.7 %fusion.161 = (bf16[1,512,5120]{2,1,0:T(8,128)(2,1)}, bf16[1,512,5120]{2,1,0:T(8,128)(2,1)}) fusion(bf16[2,512,5120]{2,1,0:T(8,128)(2,1)} %param.23), kind=kLoop, calls=%fused_computation.174 | loop fusion | bytes 20971520 | tf_op jit(solution)/shard_map/slice | solution.py:77
  93.3 4.0 fusion.78
  98.1 1.6 copy.27
  99.7 31.4 %all-gather.24.cloned.1.call-done = bf16[4096,128]{1,0:T(8,128)(2,1)} async-done(((bf16[256,128]{1,0:T(8,128)(2,1)}), bf16[4096,128]{1,0:T(8,128)(2,1)}) %all-gather.24.cloned.1.call-update) | async-done | bytes 1048592 | tf_op jit(solution)/shard_map/all_gather | solution.py:75
  131.2 11.5 %while.22 = (s32[]{:T(128)}, bf16[2,1,4,128,128]{4,3,2,1,0:T(8,128)(2,1)S(1)}, s32[2,128]{1,0:T(2,128)S(1)}, s32[2,128]{1,0:T(2,128)S(1)}, s32[4096]{0:T(1024)S(...) while((s32[]{:T(128)}, ...), condition=%wide.region_4.5_spmd.clone, body=%wide.region_1.4_spmd.clone.sunk | while | flops 1092156416 | bytes 32797828 | solution.py:45
  131.2 0.5 fusion.191
  131.7 1.8 fusion.192
  133.5 1.3 fusion.193
  134.8 2.1 fusion.194
  137.4 1.8 fusion.192
  139.2 1.3 fusion.193
  140.5 2.1 fusion.194
  142.7 5.3 fusion.62
  148.2 33.1 %reduce-scatter.5.cloned.1.call-done = bf16[32,5120]{1,0:T(8,128)(2,1)} async-done(((bf16[256,5120]{1,0:T(8,128)(2,1)}), bf16[32,5120]{1,0:T(8,128)(2,1)}) %reduce-scatter.5.cloned.1.call-update) | async-done | bytes 327696 | tf_op jit(solution)/shard_map/reduce_scatter | solution.py:79
  181.3 1.2 fusion.126
  182.5 1.8 fusion.128
  184.6 28.0 %all-gather.16.cloned.1.call-done = bf16[256,5120]{1,0:T(8,128)(2,1)} async-done(((bf16[32,5120]{1,0:T(8,128)(2,1)}), bf16[256,5120]{1,0:T(8,128)(2,1)}) %all-gather.16.cloned.1.call-update) | async-done | bytes 2621456 | tf_op jit(solution)/shard_map/all_gather | solution.py:81
  212.6 10.3 %fusion.54 = f32[256,1792]{1,0:T(8,128)S(1)} fusion(bf16[256,5120]{1,0:T(8,128)(2,1)} %all-gather.16.cloned.1.call-done, bf16[2,5120,1792]{2,1,0:T(8,128)(2,1)} %param.25), kind=kOutput, calls=%fused_computation.52 | convolution fusion | flops 4697620480 | bytes 22806528 | tf_op jit(solution)/shard_map/dot_general | solution.py:82
  222.9 20.1 %fusion.64 = bf16[256,5120]{1,0:T(8,128)(2,1)} fusion(bf16[2,1792,5120]{2,1,0:T(8,128)(2,1)} %param.27, bf16[256,5120]{1,0:T(8,128)(2,1)} %all-gather.16.cloned.1.call-done, bf16[2,5120,1792]{2,1,0:T(8,128)(2,1)} %param.26, f32[256,1792]{1,0:T(8,128)S(1)} %fusion.54), kind=kOutput, calls=%fused_computation.64 | convolution fusion | flops 9399304192 | bytes 43778048 | tf_op jit(solution)/shard_map/dot_general | solution.py:85
  243.1 32.3 %reduce-scatter.7.cloned.1.call-done = bf16[32,5120]{1,0:T(8,128)(2,1)} async-done(((bf16[256,5120]{1,0:T(8,128)(2,1)}), bf16[32,5120]{1,0:T(8,128)(2,1)}) %reduce-scatter.7.cloned.1.call-update) | async-done | bytes 327696 | tf_op jit(solution)/shard_map/reduce_scatter | solution.py:86
  275.4 1.2 fusion.130
  276.7 0.9 fusion.132
  277.6 28.2 %all-gather.18.cloned.1.call-done = bf16[256,5120]{1,0:T(8,128)(2,1)} async-done(((bf16[32,5120]{1,0:T(8,128)(2,1)}), bf16[256,5120]{1,0:T(8,128)(2,1)}) %all-gather.18.cloned.1.call-update) | async-done | bytes 2621456 | tf_op jit(solution)/shard_map/all_gather | solution.py:68
  305.8 3.1 fusion.111
  309.2 0.6 pad_maximum_fusion.4
  310.0 3.6 fusion.117
  313.9 7.9 %copy.28 = bf16[512,5120]{1,0:T(8,128)(2,1)} copy(bf16[512,5120]{0,1:T(8,128)(2,1)} %get-tuple-element.218) | data formatting | bytes 10485760 | tf_op jit(solution)/shard_map/dot_general | solution.py:69
  321.7 4.8 fusion.76
  327.3 24.4 %all-gather.20.cloned.1.call-done = bf16[4096,1,128]{0,2,1:T(8,128)(2,1)} async-done(((bf16[256,1,128]{0,2,1:T(8,128)(2,1)}), bf16[4096,1,128]{0,2,1:T(8,128)(2,1)}) %all-gather.20.cloned.1.call-update) | async-done | bytes 1048592 | tf_op jit(solution)/shard_map/all_gather | solution.py:74
  351.7 1.6 copy.31
  353.3 42.1 %all-gather.26.cloned.1.call-done = bf16[4096,128]{1,0:T(8,128)(2,1)} async-done(((bf16[256,128]{1,0:T(8,128)(2,1)}), bf16[4096,128]{1,0:T(8,128)(2,1)}) %all-gather.26.cloned.1.call-update) | async-done | bytes 1048592 | tf_op jit(solution)/shard_map/all_gather | solution.py:75
  395.5 11.5 %while.23 = (s32[]{:T(128)}, bf16[2,1,4,128,128]{4,3,2,1,0:T(8,128)(2,1)S(1)}, s32[2,128]{1,0:T(2,128)S(1)}, s32[2,128]{1,0:T(2,128)S(1)}, s32[4096]{0:T(1024)S(...) while((s32[]{:T(128)}, ...), condition=%wide.region_12.13_spmd.clone, body=%wide.region_9.12_spmd.clone.sunk | while | flops 1092156416 | bytes 32797828 | solution.py:45
  396.0 1.8 fusion.199
  397.8 1.3 fusion.200
  399.1 2.1 fusion.201
  401.7 1.8 fusion.199
  403.5 1.3 fusion.200
  404.8 2.1 fusion.201
  407.0 5.3 fusion.63
  412.4 33.2 %reduce-scatter.9.cloned.1.call-done = bf16[32,5120]{1,0:T(8,128)(2,1)} async-done(((bf16[256,5120]{1,0:T(8,128)(2,1)}), bf16[32,5120]{1,0:T(8,128)(2,1)}) %reduce-scatter.9.cloned.1.call-update) | async-done | bytes 327696 | tf_op jit(solution)/shard_map/reduce_scatter | solution.py:79
  445.5 1.2 fusion.134
  446.7 1.8 fusion.136
  448.9 27.9 %all-gather.22.cloned.1.call-done = bf16[256,5120]{1,0:T(8,128)(2,1)} async-done(((bf16[32,5120]{1,0:T(8,128)(2,1)}), bf16[256,5120]{1,0:T(8,128)(2,1)}) %all-gather.22.cloned.1.call-update) | async-done | bytes 2621456 | tf_op jit(solution)/shard_map/all_gather | solution.py:81
  476.9 13.1 %fusion.48 = f32[256,1792]{1,0:T(8,128)} fusion(bf16[256,5120]{1,0:T(8,128)(2,1)} %all-gather.22.cloned.1.call-done, bf16[2,5120,1792]{2,1,0:T(8,128)(2,1)} %param.25), kind=kOutput, calls=%fused_computation.46 | convolution fusion | flops 4697620480 | bytes 22806528 | tf_op jit(solution)/shard_map/dot_general | solution.py:82
  490.0 20.2 %fusion.67 = bf16[256,5120]{1,0:T(8,128)(2,1)} fusion(bf16[2,1792,5120]{2,1,0:T(8,128)(2,1)} %param.27, bf16[256,5120]{1,0:T(8,128)(2,1)} %all-gather.22.cloned.1.call-done, bf16[2,5120,1792]{2,1,0:T(8,128)(2,1)} %param.26, f32[256,1792]{1,0:T(8,128)} %fusion.48), kind=kOutput, calls=%fused_computation.65 | convolution fusion | flops 9399304192 | bytes 43778048 | tf_op jit(solution)/shard_map/dot_general | solution.py:85
  510.3 0.8 copy.32
  511.1 0.7 pad_maximum_fusion.2
  511.8 30.9 %reduce-scatter.11.cloned.1.call-done = bf16[32,5120]{1,0:T(8,128)(2,1)} async-done(((bf16[256,5120]{1,0:T(8,128)(2,1)}), bf16[32,5120]{1,0:T(8,128)(2,1)}) %reduce-scatter.11.cloned.1.call-update) | async-done | bytes 327696 | tf_op jit(solution)/shard_map/reduce_scatter | solution.py:86
  542.7 1.8 fusion.137
  (89 shorter events, 5.7 us)
Async XLA Ops:
  7.2 33.7 %all-gather.12.cloned.1.call-start = ((), (), s32[]{:S(2)}) async-start(), calls=%async_computation.4 | async-start | bytes 2949120 | tf_op jit(solution)/shard_map/all_gather | solution.py:68
  11.1 87.0 %all-gather.14.cloned.1.call-start = ((), (), s32[]{:S(2)}) async-start(), calls=%async_computation.5 | async-start | bytes 1114112 | tf_op jit(solution)/shard_map/all_gather | solution.py:74
  44.3 0.6 copy-start.4
  44.3 0.6 copy-start.6
  45.6 85.6 %all-gather.24.cloned.1.call-start = ((), (), s32[]{:S(2)}) async-start(), calls=%async_computation.14 | async-start | bytes 1114112 | tf_op jit(solution)/shard_map/all_gather | solution.py:75
  54.4 27.2 %copy-start.3 = (bf16[256,5120]{1,0:T(8,128)(2,1)S(1)}, bf16[256,5120]{1,0:T(8,128)(2,1)}, u32[]{:S(2)}) copy-start(bf16[256,5120]{1,0:T(8,128)(2,1)} %all-gather.12.cloned.1.call-done) | copy-start | bytes 7864324
  84.4 96.9 %reduce-scatter.5.cloned.1.call-start = ((), (), s32[]{:S(2)}) async-start(), calls=%async_computation.6 | async-start | bytes 2949120 | tf_op jit(solution)/shard_map/reduce_scatter | solution.py:79
  133.5 1.3 copy-start.12
  139.2 1.3 copy-start.12
  142.7 5.4 copy-start.10
  142.7 38.6 %copy-start = (bf16[32,5120]{1,0:T(8,128)(2,1)S(1)}, bf16[32,5120]{1,0:T(8,128)(2,1)}, u32[]{:S(2)}) copy-start(bf16[32,5120]{1,0:T(8,128)(2,1)} %param.16) | copy-start | bytes 983044
  148.1 64.5 %all-gather.16.cloned.1.call-start = ((), (), s32[]{:S(2)}) async-start(), calls=%async_computation.7 | async-start | bytes 2949120 | tf_op jit(solution)/shard_map/all_gather | solution.py:81
  184.3 91.1 %reduce-scatter.7.cloned.1.call-start = ((), (), s32[]{:S(2)}) async-start(), calls=%async_computation.8 | async-start | bytes 2949120 | tf_op jit(solution)/shard_map/reduce_scatter | solution.py:86
  222.9 52.5 %copy-start.2 = (bf16[32,5120]{1,0:T(8,128)(2,1)S(1)}, bf16[32,5120]{1,0:T(8,128)(2,1)}, u32[]{:S(2)}) copy-start(bf16[32,5120]{1,0:T(8,128)(2,1)} %reduce-scatter.5.cloned.1.call-done) | copy-start | bytes 983044
  243.0 62.8 %all-gather.18.cloned.1.call-start = ((), (), s32[]{:S(2)}) async-start(), calls=%async_computation.9 | async-start | bytes 2949120 | tf_op jit(solution)/shard_map/all_gather | solution.py:68
  277.6 74.1 %all-gather.20.cloned.1.call-start = ((), (), s32[]{:S(2)}) async-start(), calls=%async_computation.10 | async-start | bytes 1114112 | tf_op jit(solution)/shard_map/all_gather | solution.py:74
  309.9 85.5 %all-gather.26.cloned.1.call-start = ((), (), s32[]{:S(2)}) async-start(), calls=%async_computation.15 | async-start | bytes 1114112 | tf_op jit(solution)/shard_map/all_gather | solution.py:75
  313.5 132.0 %reduce-scatter.9.cloned.1.call-start = ((), (), s32[]{:S(2)}) async-start(), calls=%async_computation.11 | async-start | bytes 2949120 | tf_op jit(solution)/shard_map/reduce_scatter | solution.py:79
  397.8 1.3 copy-start.11
  403.5 1.3 copy-start.11
  412.3 64.5 %all-gather.22.cloned.1.call-start = ((), (), s32[]{:S(2)}) async-start(), calls=%async_computation.12 | async-start | bytes 2949120 | tf_op jit(solution)/shard_map/all_gather | solution.py:81
  448.6 94.1 %reduce-scatter.11.cloned.1.call-start = ((), (), s32[]{:S(2)}) async-start(), calls=%async_computation.13 | async-start | bytes 2949120 | tf_op jit(solution)/shard_map/reduce_scatter | solution.py:86
  490.0 20.3 %copy-start.5 = (bf16[256,1,64]{0,2,1:T(8,128)(2,1)S(1)}, bf16[256,1,64]{0,2,1:T(8,128)(2,1)}, u32[]{:S(2)}) copy-start(bf16[256,1,64]{0,2,1:T(8,128)(2,1)} %copy-done.4) | copy-start | bytes 98308
  490.0 20.3 %copy-start.7 = (bf16[256,1,64]{0,2,1:T(8,128)(2,1)S(1)}, bf16[256,1,64]{0,2,1:T(8,128)(2,1)}, u32[]{:S(2)}) copy-start(bf16[256,1,64]{0,2,1:T(8,128)(2,1)} %copy-done.6) | copy-start | bytes 98308
  490.0 21.1 %copy-start.8 = (bf16[256,128]{1,0:T(8,128)(2,1)S(1)}, bf16[256,128]{1,0:T(8,128)(2,1)}, u32[]{:S(2)}) copy-start(bf16[256,128]{1,0:T(8,128)(2,1)} %fusion.114) | copy-start | bytes 196612
  490.0 21.1 %copy-start.9 = (bf16[256,128]{1,0:T(8,128)(2,1)S(1)}, bf16[256,128]{1,0:T(8,128)(2,1)}, u32[]{:S(2)}) copy-start(bf16[256,128]{1,0:T(8,128)(2,1)} %fusion.117) | copy-start | bytes 196612
  490.0 52.7 %copy-start.1 = (bf16[32,5120]{1,0:T(8,128)(2,1)S(1)}, bf16[32,5120]{1,0:T(8,128)(2,1)}, u32[]{:S(2)}) copy-start(bf16[32,5120]{1,0:T(8,128)(2,1)} %reduce-scatter.9.cloned.1.call-done) | copy-start | bytes 983044
Sparse Core Ops, SparseCore 0:
  11.2 29.6 all-gather.11
  45.7 41.6 all-gather.13
  89.6 41.5 all-gather.23
  148.2 33.0 reduce-scatter.4
  184.5 28.1 all-gather.15
  243.2 32.2 reduce-scatter.6
  277.7 28.0 all-gather.17
  310.0 41.6 all-gather.19
  353.9 41.5 all-gather.25
  412.4 33.0 reduce-scatter.8
  448.7 28.1 all-gather.21
  510.4 32.2 reduce-scatter.10
where the time goes:
time: 554 us; the launch traced here: 551 us
  waiting for transfers between devices  329 us (59%)
  matrix products  111 us (20%)
  local copies, waits for them, and re-layouts  41.9 us (8%)
  blocking collectives  27.4 us (5%)
  other arithmetic  24.3 us (4%)
  between operations  15.2 us (3%)
    all_gather x2, waiting for transfers between devices, device_fn(): v_keys = lax.all_gather(v_rows, 'sp', axis=0, tiled=True)  73.6 us
    reduce_scatter x2, waiting for transfers between devices, device_fn(): attn_res = lax.psum_scatter(part_sum, 'tp', scatter_dimension=0, tiled=True)  66.3 us
    reduce_scatter x2, waiting for transfers between devices, device_fn(): mlp_res = lax.psum_scatter(down_part, 'tp', scatter_dimension=0, tiled=True)  63.2 us
    all_gather x2, waiting for transfers between devices, device_fn(): lax.all_gather(rms_norm(hidden_mid, mlp_gain[layer_idx]), 'tp', axis=0, t...  55.9 us
    all_gather x2, waiting for transfers between devices, device_fn(): lax.all_gather(rms_norm(hidden, attn_gain[layer_idx]), 'tp', axis=0, tile...  45.8 us
    dot_general x2, matrix products, device_fn(): jnp.dot(act_vals, w_down[layer_idx], preferred_element_type=jnp.float32)  40.3 us
    dot_general x3, local copies, waits for them, and re-layouts, device_fn(): jnp.dot(normed, w_q[layer_idx], preferred_element_type=jnp.float32)  24.6 us
    all_gather x2, waiting for transfers between devices, device_fn(): k_keys = lax.all_gather(k_rows, 'sp', axis=0, tiled=True)  24.4 us
  transfers between devices with their start and end apart: 12, of which 11 were waited for; matrix products, arithmetic and copies ran while one was open for 10% of the time, Pallas kernels for 0%

commit v1 on v0

--- a/solution.py
+++ b/solution.py
@@ -1,13 +1,329 @@
+import functools
 import math
 import jax
 import jax.numpy as jnp
 from jax import lax
+from jax.experimental import pallas as pl
+from jax.experimental.pallas import tpu as pltpu
 from jax.sharding import PartitionSpec as P
 
 HEAD_DIM = 128
 ROPE_BASE = 1e4
 NORM_EPS = 1e-5
 SCORE_SCALE = HEAD_DIM ** -0.5
+NX = 4
+AG_AHEAD = 4
+AG_LAG_O = 3
+AG_LAG = 5
+RS_LAG_D = 2
+RS_LAG_T = 5
+RS_LAG_F = 8
+WG_SLOTS = 4
+WD_SLOTS = 4
+MESH = pl.DeviceIdType.MESH
+F32 = jnp.float32
+BF16 = jnp.bfloat16
+
+
+class Ring:
+    def __init__(self):
+        tp = lax.axis_index('tp')
+        self.tp = tp
+        self.x = lax.div(tp, 2)
+        self.c = lax.rem(tp, 2)
+
+    def dev(self, dx, same_core=True):
+        core = self.c if same_core else 1 - self.c
+        return {'tp': 2 * self.at(dx) + core}
+
+    def at(self, dx):
+        return lax.rem(self.x + dx + NX, NX)
+
+
+def col(ref, j, width):
+    return ref.at[:, pl.ds(pl.multiple_of(j * width, width), width)]
+
+
+class Gather:
+    def __init__(self, ring, buf, send, recv, rows, nch):
+        self.g, self.buf, self.send, self.recv, self.rows, self.nch = ring, buf, send, recv, rows, nch
+
+    def block(self, j, dx, same_core):
+        core = self.g.c if same_core else 1 - self.g.c
+        r = pl.multiple_of((2 * self.g.at(dx) + core) * self.rows, self.rows)
+        return self.buf.at[j, pl.ds(r, self.rows), :]
+
+    def copy(self, j, kind, dx, to):
+        ref = self.block(j, dx, True)
+        return pltpu.make_async_remote_copy(src_ref=ref, dst_ref=ref, send_sem=self.send.at[kind, j], recv_sem=self.recv.at[kind, j],
+                                            device_id=to, device_id_type=MESH)
+
+    def arrival(self, j, kind, dx, same_core):
+        ref = self.block(j, dx, same_core)
+        return pltpu.make_async_remote_copy(src_ref=ref, dst_ref=ref, send_sem=self.send.at[kind, j], recv_sem=self.recv.at[kind, j],
+                                            device_id=self.g.dev(0, False), device_id_type=MESH)
+
+    def start(self, j):
+        self.copy(j, 0, 0, self.g.dev(1)).start()
+        self.copy(j, 1, 0, self.g.dev(-1)).start()
+        self.copy(j, 3, 0, self.g.dev(0, False)).start()
+
+    def forward(self, j):
+        self.arrival(j, 0, -1, True).wait_recv()
+        self.arrival(j, 1, 1, True).wait_recv()
+        way = 1 - 2 * lax.rem(j, 2)
+        self.copy(j, 2, -way, self.g.dev(way)).start()
+        self.copy(j, 4, -1, self.g.dev(0, False)).start()
+        self.copy(j, 5, 1, self.g.dev(0, False)).start()
+
+    def forward_far(self, j):
+        self.arrival(j, 2, 2, True).wait_recv()
+        self.copy(j, 6, 2, self.g.dev(0, False)).start()
+
+    def whole(self, j):
+        self.arrival(j, 3, 0, False).wait_recv()
+        self.arrival(j, 4, -1, False).wait_recv()
+        self.arrival(j, 5, 1, False).wait_recv()
+        self.arrival(j, 6, 2, False).wait_recv()
+
+    def drain(self):
+        def body(j, _):
+            for kind in range(7):
+                self.arrival(j, kind, 0, True).wait_send()
+            return 0
+        lax.fori_loop(0, self.nch, body, 0)
+
+    def run(self, use, last=None):
+        nch = self.nch
+        for j in range(min(AG_AHEAD, nch)):
+            self.start(j)
+
+        def body(s, _):
+            @pl.when(s < nch)
+            def _():
+                self.forward(s)
+
+            @pl.when(s + AG_AHEAD < nch)
+            def _():
+                self.start(s + AG_AHEAD)
+
+            @pl.when((s >= AG_LAG_O) & (s - AG_LAG_O < nch))
+            def _():
+                self.forward_far(s - AG_LAG_O)
+
+            @pl.when(s >= AG_LAG)
+            def _():
+                self.whole(s - AG_LAG)
+                use(s - AG_LAG)
+            return 0
+        stop = nch if last is None else nch - 1
+        lax.fori_loop(0, stop + AG_LAG, body, 0)
+        if last is not None:
+            self.whole(nch - 1)
+            last()
+        self.drain()
+
+
+class Scatter:
+    def __init__(self, ring, part, pair, passing, ends, own, out, send, recv, nch):
+        self.g, self.part, self.pair, self.passing, self.ends, self.own, self.out = ring, part, pair, passing, ends, own, out
+        self.send, self.recv, self.nch = send, recv, nch
+
+    def remote(self, j, kind, src, dst, to):
+        return pltpu.make_async_remote_copy(src_ref=src, dst_ref=dst, send_sem=self.send.at[kind, j], recv_sem=self.recv.at[kind, j],
+                                            device_id=to, device_id_type=MESH)
+
+    def pair_copy(self, j):
+        return self.remote(j, 0, self.part.at[j, :, 1 - self.g.c], self.pair.at[j], self.g.dev(0, False))
+
+    def far_copy(self, j):
+        way = 1 - 2 * lax.rem(j, 2)
+        return self.remote(j, 1, self.out.at[j, 2], self.passing.at[j], self.g.dev(way))
+
+    def near_copy(self, j, side):
+        return self.remote(j, 2 + side, self.out.at[j, side], self.ends.at[j, side], self.g.dev(1 - 2 * side))
+
+    def near_now(self, j, odd):
+        self.near_copy(j, 1 - odd).start()
+
+    def stage_pair(self, j):
+        self.pair_copy(j).wait_recv()
+        g = self.g
+
+        def both(dx):
+            xx = g.at(dx)
+            return self.part[j, xx, g.c].astype(F32) + self.pair[j, xx].astype(F32)
+        self.out[j, 2] = both(2).astype(BF16)
+        self.far_copy(j).start()
+        self.out[j, 0] = both(1).astype(BF16)
+        self.out[j, 1] = both(-1).astype(BF16)
+        side = 1 - lax.rem(j, 2)
+        pltpu.make_async_remote_copy(src_ref=self.out.at[j, side], dst_ref=self.ends.at[j, side], send_sem=self.send.at[2, j],
+                                     recv_sem=self.recv.at[2, j], device_id=g.dev(1 - 2 * side), device_id_type=MESH).start()
+        self.own[j] = both(0)
+
+    def stage_pass(self, j):
+        g = self.g
+        self.far_copy(j).wait_recv()
+        side = lax.rem(j, 2)
+        self.out[j, side] = (self.out[j, side].astype(F32) + self.passing[j].astype(F32)).astype(BF16)
+        pltpu.make_async_remote_copy(src_ref=self.out.at[j, side], dst_ref=self.ends.at[j, side], send_sem=self.send.at[3, j],
+                                     recv_sem=self.recv.at[3, j], device_id=g.dev(1 - 2 * side), device_id_type=MESH).start()
+
+    def stage_end(self, j):
+        for kind in (2, 3):
+            self.remote(j, kind, self.ends.at[j, 0], self.ends.at[j, 0], self.g.dev(1)).wait_recv()
+        return self.own[j] + self.ends[j, 0].astype(F32) + self.ends[j, 1].astype(F32)
+
+    def drain(self):
+        def body(j, _):
+            self.pair_copy(j).wait_send()
+            for kind in (1, 2, 3):
+                self.remote(j, kind, self.ends.at[j, 0], self.ends.at[j, 0], self.g.dev(1)).wait_send()
+            return 0
+        lax.fori_loop(0, self.nch, body, 0)
+
+    def run(self, compute, finish):
+        nch = self.nch
+
+        def body(s, _):
+            @pl.when(s < nch)
+            def _():
+                self.part[s] = compute(s)
+                self.pair_copy(s).start()
+
+            @pl.when((s >= RS_LAG_D) & (s - RS_LAG_D < nch))
+            def _():
+                self.stage_pair(s - RS_LAG_D)
+
+            @pl.when((s >= RS_LAG_T) & (s - RS_LAG_T < nch))
+            def _():
+                self.stage_pass(s - RS_LAG_T)
+
+            @pl.when(s >= RS_LAG_F)
+            def _():
+                j = s - RS_LAG_F
+                finish(j, self.stage_end(j))
+            return 0
+        lax.fori_loop(0, nch + RS_LAG_F, body, 0)
+        self.drain()
+
+
+def enter(peers):
+    barrier = pltpu.get_barrier_semaphore()
+    for dev in peers:
+        pl.semaphore_signal(barrier, inc=1, device_id=dev, device_id_type=MESH)
+    pl.semaphore_wait(barrier, len(peers))
+
+
+def mlp_kernel(layer, dims, h_hbm, gain_ref, wg_hbm, wu_hbm, wd_hbm, out_ref,
+               h_ref, nbuf, acc_g, acc_u, act, wgu, wd, part, pair, passing, ends, own, outs,
+               h_sem, w_sem, d_sem, ag_send, ag_recv, rs_send, rs_recv):
+    rows, d_model, units, nch = dims
+    cw = d_model // nch
+    g = Ring()
+    h_in = pltpu.make_async_copy(h_hbm, h_ref, h_sem)
+    h_in.start()
+
+    def gu_copy(j, k):
+        slot = lax.rem(j, WG_SLOTS)
+        src = (wg_hbm, wu_hbm)[k]
+        return pltpu.make_async_copy(src.at[layer, pl.ds(pl.multiple_of(j * cw, cw), cw), :], wgu.at[slot, k], w_sem.at[slot, k])
+
+    def d_copy(j):
+        slot = lax.rem(j, WD_SLOTS)
+        return pltpu.make_async_copy(wd_hbm.at[layer, :, pl.ds(pl.multiple_of(j * cw, cw), cw)], wd.at[slot], d_sem.at[slot])
+    for j in range(WG_SLOTS):
+        gu_copy(j, 0).start()
+        gu_copy(j, 1).start()
+    for j in range(WD_SLOTS):
+        d_copy(j).start()
+    enter([g.dev(1), g.dev(-1), g.dev(0, False)])
+    h_in.wait()
+
+    h32 = h_ref[...].astype(F32)
+    inv = lax.rsqrt(jnp.mean(h32 * h32, axis=-1, keepdims=True) + NORM_EPS)
+    me = pl.ds(pl.multiple_of(g.tp * rows, rows), rows)
+    for j in range(nch):
+        sl = slice(j * cw, (j + 1) * cw)
+        nbuf[j, me, :] = (h_ref[:, sl].astype(F32) * inv * gain_ref[layer:layer + 1, sl].astype(F32)).astype(BF16)
+    acc_g[...] = jnp.zeros_like(acc_g)
+    acc_u[...] = jnp.zeros_like(acc_u)
+
+    def gate_up(j):
+        slot = lax.rem(j, WG_SLOTS)
+        for k, acc in ((0, acc_g), (1, acc_u)):
+            gu_copy(j, k).wait()
+            acc[...] += jnp.dot(nbuf[j], wgu[slot, k], preferred_element_type=F32)
+
+            @pl.when(j + WG_SLOTS < nch)
+            def _():
+                gu_copy(j + WG_SLOTS, k).start()
+
+    def gate_up_last():
+        j = nch - 1
+        slot = j % WG_SLOTS
+        gu_copy(j, 0).wait()
+        gu_copy(j, 1).wait()
+        step = min(256, units)
+        for t in range(0, units, step):
+            sl = slice(t, t + step)
+            gate = acc_g[:, sl] + jnp.dot(nbuf[j], wgu[slot, 0, :, sl], preferred_element_type=F32)
+            up = acc_u[:, sl] + jnp.dot(nbuf[j], wgu[slot, 1, :, sl], preferred_element_type=F32)
+            act[:, sl] = (gate * jax.nn.sigmoid(gate) * up).astype(BF16)
+
+    Gather(g, nbuf, ag_send, ag_recv, rows, nch).run(gate_up, gate_up_last)
+
+    def down(j):
+        d_copy(j).wait()
+        slot = lax.rem(j, WD_SLOTS)
+        res = jnp.dot(act[...], wd[slot], preferred_element_type=F32).astype(BF16)
+
+        @pl.when(j + WD_SLOTS < nch)
+        def _():
+            d_copy(j + WD_SLOTS).start()
+        return res.reshape(NX, 2, rows, cw)
+
+    def finish(j, total):
+        h_col = col(h_ref, j, cw)
+        col(out_ref, j, cw)[...] = (h_col[...].astype(F32) + total.astype(BF16).astype(F32)).astype(BF16)
+
+    Scatter(g, part, pair, passing, ends, own, outs, rs_send, rs_recv, nch).run(down, finish)
+
+
+def mlp_call(layer, hidden, gain, w_gate, w_up, w_down, nch=10):
+    rows, d_model = hidden.shape
+    units = w_gate.shape[2]
+    cw = d_model // nch
+    tokens = rows * NX * 2
+    any_spec = pl.BlockSpec(memory_space=pl.ANY)
+    vmem = pl.BlockSpec(memory_space=pltpu.VMEM)
+    dma = pltpu.SemaphoreType.DMA
+    return pl.pallas_call(
+        functools.partial(mlp_kernel, layer, (rows, d_model, units, nch)),
+        out_shape=jax.ShapeDtypeStruct((rows, d_model), BF16),
+        in_specs=[any_spec, vmem, any_spec, any_spec, any_spec],
+        out_specs=vmem,
+        scratch_shapes=[
+            pltpu.VMEM((rows, d_model), BF16),
+            pltpu.VMEM((nch, tokens, cw), BF16),
+            pltpu.VMEM((tokens, units), F32),
+            pltpu.VMEM((tokens, units), F32),
+            pltpu.VMEM((tokens, units), BF16),
+            pltpu.VMEM((WG_SLOTS, 2, cw, units), BF16),
+            pltpu.VMEM((WD_SLOTS, units, cw), BF16),
+            pltpu.VMEM((nch, NX, 2, rows, cw), BF16),
+            pltpu.VMEM((nch, NX, rows, cw), BF16),
+            pltpu.VMEM((nch, rows, cw), BF16),
+            pltpu.VMEM((nch, 2, rows, cw), BF16),
+            pltpu.VMEM((nch, rows, cw), F32),
+            pltpu.VMEM((nch, 3, rows, cw), BF16),
+            dma, dma((WG_SLOTS, 2)), dma((WD_SLOTS,)),
+            dma((7, nch)), dma((7, nch)), dma((4, nch)), dma((4, nch)),
+        ],
+        compiler_params=pltpu.CompilerParams(collective_id=0, has_side_effects=True, vmem_limit_bytes=62 * 1024 * 1024),
+        name='mlp',
+    )(hidden, gain, w_gate, w_up, w_down)
 
 
 def rms_norm(hidden, gain_vec):
@@ -78,13 +394,7 @@
             part_sum = jnp.einsum('nkgqd,kgdm->nqm', att_out, wo_heads, preferred_element_type=jnp.float32).astype(jnp.bfloat16).reshape(n_rows, model_dim)
             attn_res = lax.psum_scatter(part_sum, 'tp', scatter_dimension=0, tiled=True)
             hidden_mid = (hidden.astype(jnp.float32) + attn_res.astype(jnp.float32)).astype(jnp.bfloat16)
-            normed_mlp = lax.all_gather(rms_norm(hidden_mid, mlp_gain[layer_idx]), 'tp', axis=0, tiled=True)
-            gate_lin = jnp.dot(normed_mlp, w_gate[layer_idx], preferred_element_type=jnp.float32)
-            up_lin = jnp.dot(normed_mlp, w_up[layer_idx], preferred_element_type=jnp.float32)
-            act_vals = (jax.nn.silu(gate_lin) * up_lin).astype(jnp.bfloat16)
-            down_part = jnp.dot(act_vals, w_down[layer_idx], preferred_element_type=jnp.float32).astype(jnp.bfloat16)
-            mlp_res = lax.psum_scatter(down_part, 'tp', scatter_dimension=0, tiled=True)
-            hidden = (hidden_mid.astype(jnp.float32) + mlp_res.astype(jnp.float32)).astype(jnp.bfloat16)
+            hidden = mlp_call(layer_idx, hidden_mid, mlp_gain, w_gate, w_up, w_down)
             k_list.append(k_rows)
             v_list.append(v_rows)
         return hidden, jnp.stack(k_list), jnp.stack(v_list)

time: 554 us -> 470 us (0.85)
  waiting for transfers between devices: 329 us -> 211 us
  Pallas kernels: 0 us -> 103 us
  matrix products: 111 us -> 46.6 us
    pallas_call x0 -> x2, Pallas kernels: none -> 103 us  [mlp_call(): pl.pallas_call(functools.partial(mlp_kernel, layer, (rows, d_model, units...]
    dot_general x4 -> x0, matrix products: 63.8 us -> none  [the longest x2 40.3 us: device_fn(): jnp.dot(act_vals, w_down[layer_idx], preferred_element_type=jnp.float32)]
    reduce_scatter x2 -> x0, waiting for transfers between devices: 63.2 us -> none  [device_fn(): mlp_res = lax.psum_scatter(down_part, 'tp', scatter_dimension=0, tiled=True)]
    all_gather x2 -> x0, waiting for transfers between devices: 55.9 us -> none  [device_fn(): lax.all_gather(rms_norm(hidden_mid, mlp_gain[layer_idx]), 'tp', axis=0, t...]
  transfers between devices with their start and end apart: 12 -> 8, of which waited for: 11 -> 7; matrix products, arithmetic and copies ran while one was open for 10% -> 12% of each run, Pallas kernels for 0% -> 0%
where the time goes in v1:
time: 470 us; the launch traced here: 469 us
  waiting for transfers between devices  211 us (45%)
  Pallas kernels  103 us (22%)
  matrix products  46.6 us (10%)
  local copies, waits for them, and re-layouts  43.8 us (9%)
  blocking collectives  27.4 us (6%)
  other arithmetic  21 us (4%)
  between operations  15.1 us (3%)
    pallas_call x2, Pallas kernels, mlp_call(): pl.pallas_call(functools.partial(mlp_kernel, layer, (rows, d_model, units...  103 us
    all_gather x2, waiting for transfers between devices, device_fn(): v_keys = lax.all_gather(v_rows, 'sp', axis=0, tiled=True)  74.2 us
    reduce_scatter x2, waiting for transfers between devices, device_fn(): attn_res = lax.psum_scatter(part_sum, 'tp', scatter_dimension=0, tiled=True)  64.7 us
    all_gather x2, waiting for transfers between devices, device_fn(): lax.all_gather(rms_norm(hidden, attn_gain[layer_idx]), 'tp', axis=0, tile...  46.5 us
    all_gather x2, waiting for transfers between devices, device_fn(): k_keys = lax.all_gather(k_rows, 'sp', axis=0, tiled=True)  25.4 us
    dot_general x3, local copies, waits for them, and re-layouts, device_fn(): jnp.dot(normed, w_q[layer_idx], preferred_element_type=jnp.float32)  24.8 us
    all_gather x1, blocking collectives, device_fn(): key_seg = lax.all_gather(row_seg, 'sp', tiled=True)  18.9 us
    dot_general x2, matrix products, device_fn(): jnp.einsum('nkgqd,kgdm->nqm', att_out, wo_heads, preferred_element_type=j...  10.7 us
  transfers between devices with their start and end apart: 8, of which 7 were waited for; matrix products, arithmetic and copies ran while one was open for 12% of the time, Pallas kernels for 0%

profile of v1, /device:TPU:1, one launch (start us, length us, event | category | flops | bytes accessed | tf_op | source)
XLA Modules:
  0.0 468.6 jit_solution(16063095300604917369)
XLA Ops:
  7.2 0.8 slice_convert_fusion
  8.1 1.1 fusion.74
  9.2 1.9 fusion.76
  11.1 1.2 dynamic-slice
  13.0 0.9 dynamic-update-slice
  13.9 0.8 dynamic-update-slice.1
  14.7 8.5 %all-reduce.2 = (s32[256]{0:T(256)S(1)}, s32[256]{0:T(256)S(1)}) all-reduce(s32[256]{0:T(256)S(1)} %dynamic-update-slice, s32[256]{0:T(256)S(1)} %dynamic-update-slice.1), channel_id=1, replica_groups=mesh['dp'=1,'sp'=16,'tp'=8] {'tp'}, use_global_device_ids=true, to_apply=%add | all-reduce | flops 512 | bytes 4096
  23.3 17.6 %all-gather.10.cloned.1.call-done = bf16[256,5120]{1,0:T(8,128)(2,1)} async-done(((bf16[32,5120]{1,0:T(8,128)(2,1)}), bf16[256,5120]{1,0:T(8,128)(2,1)}) %all-gather.10.cloned.1.call-update) | async-done | bytes 2621456 | tf_op jit(solution)/shard_map/all_gather | solution.py:384
  40.9 3.1 fusion.62
  44.0 0.3 fusion.93
  44.3 0.6 copy-done.4
  44.9 0.6 pad_maximum_fusion.3
  45.6 8.7 %slice_bitcast_fusion = (bf16[512,5120]{0,1:T(8,128)(2,1)}, bf16[512,5120]{0,1:T(8,128)(2,1)}) fusion(bf16[2,5120,512]{2,1,0:T(8,128)(2,1)} %param.20), kind=kLoop, calls=%fused_computation.46 | loop fusion | bytes 20971520 | tf_op jit(solution)/shard_map/dot_general | solution.py:385
  54.3 8.0 %copy.24 = bf16[512,5120]{1,0:T(8,128)(2,1)} copy(bf16[512,5120]{0,1:T(8,128)(2,1)} %get-tuple-element.216) | data formatting | bytes 10485760 | tf_op jit(solution)/shard_map/dot_general | solution.py:385
  62.3 18.9 %all-gather.2 = s32[16,1,256]{2,1,0:T(1,128)S(1)} all-gather(s32[1,1,256]{2,1,0:T(1,128)S(1)} %bitcast.209), channel_id=1, replica_groups=mesh['dp'=1,'sp'=16,'tp'=8] {'sp'}, dimensions={0}, use_global_device_ids=true | all-gather | bytes 17408 | tf_op jit(solution)/shard_map/all_gather | solution.py:378
  81.3 0.3 multiply_cosine_fusion.1
  81.6 2.8 fusion.68
  84.6 8.7 %fusion.102 = (bf16[1,512,5120]{2,1,0:T(8,128)(2,1)}, bf16[1,512,5120]{2,1,0:T(8,128)(2,1)}) fusion(bf16[2,512,5120]{2,1,0:T(8,128)(2,1)} %param.23), kind=kLoop, calls=%fused_computation.122 | loop fusion | bytes 20971520 | tf_op jit(solution)/shard_map/slice | solution.py:393
  93.3 4.0 fusion.48
  98.1 1.6 copy.27
  99.7 31.5 %all-gather.18.cloned.1.call-done = bf16[4096,128]{1,0:T(8,128)(2,1)} async-done(((bf16[256,128]{1,0:T(8,128)(2,1)}), bf16[4096,128]{1,0:T(8,128)(2,1)}) %all-gather.18.cloned.1.call-update) | async-done | bytes 1048592 | tf_op jit(solution)/shard_map/all_gather | solution.py:391
  131.2 11.5 %while.22 = (s32[]{:T(128)}, bf16[2,1,4,128,128]{4,3,2,1,0:T(8,128)(2,1)S(1)}, s32[2,128]{1,0:T(2,128)S(1)}, s32[2,128]{1,0:T(2,128)S(1)}, s32[4096]{0:T(1024)S(...) while((s32[]{:T(128)}, ...), condition=%wide.region_4.5_spmd.clone, body=%wide.region_1.4_spmd.clone.sunk | while | flops 1092156416 | bytes 32797828 | solution.py:361
  131.2 0.5 fusion.128
  131.7 1.8 fusion.129
  133.5 1.3 fusion.130
  134.8 2.1 fusion.131
  137.0 0.5 fusion.128
  137.4 1.8 fusion.129
  139.2 1.3 fusion.130
  140.5 2.1 fusion.131
  142.7 5.4 %fusion.44 = bf16[2,128,5120]{2,1,0:T(8,128)(2,1)} fusion(bf16[4,128,5120,1]{2,1,0,3:T(8,128)(2,1)} %bitcast.195, bf16[2,1,4,128,128]{4,3,2,1,0:T(8,128)(2,1)S(1)} %get-tuple-element.97), kind=kOutput, calls=%fused_computation.44 | convolution fusion | flops 1343488000 | bytes 8126464 | tf_op jit(solution)/shard_map/nkgqd,kgdm->nqm/dot_general | solution.py:394
  148.1 0.3 all-gather.14.cloned.1.call-start
  148.3 32.9 %reduce-scatter.3.cloned.1.call-done = bf16[32,5120]{1,0:T(8,128)(2,1)} async-done(((bf16[256,5120]{1,0:T(8,128)(2,1)}), bf16[32,5120]{1,0:T(8,128)(2,1)}) %reduce-scatter.3.cloned.1.call-update) | async-done | bytes 327696 | tf_op jit(solution)/shard_map/reduce_scatter | solution.py:395
  181.3 1.8 fusion.77.h_hbm
  183.0 51.3 %mlp.2 = bf16[32,5120]{1,0:T(8,128)(2,1)} custom-call(bf16[32,5120]{1,0:T(8,128)(2,1)} %fusion.77.h_hbm, bf16[2,5120]{1,0:T(2,128)(2,1)} %gain_ref.3, bf16[2,5120,1792]{2,1,0:T(8,128)(2,1)} %wg_hbm.3, bf16[2,5120,1792]{2,1,0:T(8,128)(2,1)} %wu_hbm.3, bf16[2,1792,5120]{2,1,0:T(8,128)(2,1)} %wd_hbm.3), custom_call_target="tpu_custom_call" | custom-call | tf_op jit(solution)/shard_map/mlp/pallas_call | solution.py:302
  234.4 1.3 fusion.78
  235.7 1.9 fusion.80
  237.6 28.9 %all-gather.14.cloned.1.call-done = bf16[256,5120]{1,0:T(8,128)(2,1)} async-done(((bf16[32,5120]{1,0:T(8,128)(2,1)}), bf16[256,5120]{1,0:T(8,128)(2,1)}) %all-gather.14.cloned.1.call-update) | async-done | bytes 2621456 | tf_op jit(solution)/shard_map/all_gather | solution.py:384
  266.6 3.1 fusion.65
  269.7 0.3 fusion.97
  270.0 0.6 pad_maximum_fusion.4
  270.7 3.2 fusion.71
  274.0 0.3 reduce-scatter.5.cloned.1.call-start
  274.3 8.1 %copy.28 = bf16[512,5120]{1,0:T(8,128)(2,1)} copy(bf16[512,5120]{0,1:T(8,128)(2,1)} %get-tuple-element.215) | data formatting | bytes 10485760 | tf_op jit(solution)/shard_map/dot_general | solution.py:385
  282.3 4.0 fusion.46
  287.1 25.4 %all-gather.16.cloned.1.call-done = bf16[4096,1,128]{0,2,1:T(8,128)(2,1)} async-done(((bf16[256,1,128]{0,2,1:T(8,128)(2,1)}), bf16[4096,1,128]{0,2,1:T(8,128)(2,1)}) %all-gather.16.cloned.1.call-update) | async-done | bytes 1048592 | tf_op jit(solution)/shard_map/all_gather | solution.py:390
  312.5 1.6 copy.31
  314.1 42.7 %all-gather.20.cloned.1.call-done = bf16[4096,128]{1,0:T(8,128)(2,1)} async-done(((bf16[256,128]{1,0:T(8,128)(2,1)}), bf16[4096,128]{1,0:T(8,128)(2,1)}) %all-gather.20.cloned.1.call-update) | async-done | bytes 1048592 | tf_op jit(solution)/shard_map/all_gather | solution.py:391
  356.8 11.4 %while.23 = (s32[]{:T(128)}, bf16[2,1,4,128,128]{4,3,2,1,0:T(8,128)(2,1)S(1)}, s32[2,128]{1,0:T(2,128)S(1)}, s32[2,128]{1,0:T(2,128)S(1)}, s32[4096]{0:T(1024)S(...) while((s32[]{:T(128)}, ...), condition=%wide.region_10.11_spmd.clone, body=%wide.region_7.10_spmd.clone.sunk | while | flops 1092156416 | bytes 32797828 | solution.py:361
  356.8 0.5 fusion.135
  357.3 1.8 fusion.136
  359.1 1.3 fusion.137
  360.4 2.1 fusion.138
  362.6 0.5 fusion.135
  363.0 1.8 fusion.136
  364.8 1.3 fusion.137
  366.1 2.1 fusion.138
  368.3 5.4 %fusion.45 = bf16[2,128,5120]{2,1,0:T(8,128)(2,1)} fusion(bf16[4,128,5120,1]{2,1,0,3:T(8,128)(2,1)} %bitcast.194, bf16[2,1,4,128,128]{4,3,2,1,0:T(8,128)(2,1)S(1)} %get-tuple-element.98), kind=kOutput, calls=%fused_computation.45 | convolution fusion | flops 1343488000 | bytes 8126464 | tf_op jit(solution)/shard_map/nkgqd,kgdm->nqm/dot_general | solution.py:394
  373.7 0.8 copy.32
  374.5 0.7 pad_maximum_fusion.2
  375.2 31.7 %reduce-scatter.5.cloned.1.call-done = bf16[32,5120]{1,0:T(8,128)(2,1)} async-done(((bf16[256,5120]{1,0:T(8,128)(2,1)}), bf16[32,5120]{1,0:T(8,128)(2,1)}) %reduce-scatter.5.cloned.1.call-update) | async-done | bytes 327696 | tf_op jit(solution)/shard_map/reduce_scatter | solution.py:395
  406.9 1.8 fusion.81.h_hbm
  408.7 51.4 %mlp.3 = bf16[32,5120]{1,0:T(8,128)(2,1)} custom-call(bf16[32,5120]{1,0:T(8,128)(2,1)} %fusion.81.h_hbm, bf16[2,5120]{1,0:T(2,128)(2,1)} %gain_ref.3, bf16[2,5120,1792]{2,1,0:T(8,128)(2,1)} %wg_hbm.3, bf16[2,5120,1792]{2,1,0:T(8,128)(2,1)} %wu_hbm.3, bf16[2,1792,5120]{2,1,0:T(8,128)(2,1)} %wd_hbm.3), custom_call_target="tpu_custom_call" | custom-call | tf_op jit(solution)/shard_map/mlp/pallas_call | solution.py:302
  460.1 1.7 copy.55
  (70 shorter events, 2.2 us)
Async XLA Ops:
  7.2 33.7 %all-gather.10.cloned.1.call-start = ((), (), s32[]{:S(2)}) async-start(), calls=%async_computation.2 | async-start | bytes 2949120 | tf_op jit(solution)/shard_map/all_gather | solution.py:384
  11.1 87.0 %all-gather.12.cloned.1.call-start = ((), (), s32[]{:S(2)}) async-start(), calls=%async_computation.3 | async-start | bytes 1114112 | tf_op jit(solution)/shard_map/all_gather | solution.py:390
  44.3 0.6 copy-start.4
  44.3 0.6 copy-start.6
  45.6 85.6 %all-gather.18.cloned.1.call-start = ((), (), s32[]{:S(2)}) async-start(), calls=%async_computation.8 | async-start | bytes 1114112 | tf_op jit(solution)/shard_map/all_gather | solution.py:391
  54.3 27.2 %copy-start.2 = (bf16[256,5120]{1,0:T(8,128)(2,1)S(1)}, bf16[256,5120]{1,0:T(8,128)(2,1)}, u32[]{:S(2)}) copy-start(bf16[256,5120]{1,0:T(8,128)(2,1)} %all-gather.10.cloned.1.call-done) | copy-start | bytes 7864324
  84.4 96.9 %reduce-scatter.3.cloned.1.call-start = ((), (), s32[]{:S(2)}) async-start(), calls=%async_computation.4 | async-start | bytes 2949120 | tf_op jit(solution)/shard_map/reduce_scatter | solution.py:395
  133.5 1.3 copy-start.12
  139.2 1.3 copy-start.12
  142.7 38.6 %copy-start.1 = (bf16[32,5120]{1,0:T(8,128)(2,1)S(1)}, bf16[32,5120]{1,0:T(8,128)(2,1)}, u32[]{:S(2)}) copy-start(bf16[32,5120]{1,0:T(8,128)(2,1)} %param.16) | copy-start | bytes 983044
  148.1 118.5 %all-gather.14.cloned.1.call-start = ((), (), s32[]{:S(2)}) async-start(), calls=%async_computation.5 | async-start | bytes 2949120 | tf_op jit(solution)/shard_map/all_gather | solution.py:384
  234.4 36.3 %copy-start.10 = (bf16[2,5120,128]{2,1,0:T(8,128)(2,1)S(1)}, bf16[2,5120,128]{2,1,0:T(8,128)(2,1)}, u32[]{:S(2)}) copy-start(bf16[2,5120,128]{2,1,0:T(8,128)(2,1)} %param.22) | copy-start | bytes 7864324
  237.6 74.9 %all-gather.16.cloned.1.call-start = ((), (), s32[]{:S(2)}) async-start(), calls=%async_computation.6 | async-start | bytes 1114112 | tf_op jit(solution)/shard_map/all_gather | solution.py:390
  270.7 86.1 %all-gather.20.cloned.1.call-start = ((), (), s32[]{:S(2)}) async-start(), calls=%async_computation.9 | async-start | bytes 1114112 | tf_op jit(solution)/shard_map/all_gather | solution.py:391
  274.0 133.0 %reduce-scatter.5.cloned.1.call-start = ((), (), s32[]{:S(2)}) async-start(), calls=%async_computation.7 | async-start | bytes 2949120 | tf_op jit(solution)/shard_map/reduce_scatter | solution.py:395
  274.3 8.1 %copy-start.3 = (bf16[256,5120]{1,0:T(8,128)(2,1)S(1)}, bf16[256,5120]{1,0:T(8,128)(2,1)}, u32[]{:S(2)}) copy-start(bf16[256,5120]{1,0:T(8,128)(2,1)} %all-gather.14.cloned.1.call-done) | copy-start | bytes 7864324
  359.1 1.3 copy-start.11
  364.8 1.3 copy-start.11
  368.2 5.5 %copy-start.5 = (bf16[256,1,64]{0,2,1:T(8,128)(2,1)S(1)}, bf16[256,1,64]{0,2,1:T(8,128)(2,1)}, u32[]{:S(2)}) copy-start(bf16[256,1,64]{0,2,1:T(8,128)(2,1)} %copy-done.4) | copy-start | bytes 98308
  368.3 5.5 %copy-start.7 = (bf16[256,1,64]{0,2,1:T(8,128)(2,1)S(1)}, bf16[256,1,64]{0,2,1:T(8,128)(2,1)}, u32[]{:S(2)}) copy-start(bf16[256,1,64]{0,2,1:T(8,128)(2,1)} %copy-done.6) | copy-start | bytes 98308
  368.3 6.2 %copy-start.8 = (bf16[256,128]{1,0:T(8,128)(2,1)S(1)}, bf16[256,128]{1,0:T(8,128)(2,1)}, u32[]{:S(2)}) copy-start(bf16[256,128]{1,0:T(8,128)(2,1)} %fusion.68) | copy-start | bytes 196612
  368.3 6.2 %copy-start.9 = (bf16[256,128]{1,0:T(8,128)(2,1)S(1)}, bf16[256,128]{1,0:T(8,128)(2,1)}, u32[]{:S(2)}) copy-start(bf16[256,128]{1,0:T(8,128)(2,1)} %fusion.71) | copy-start | bytes 196612
  368.3 38.6 %copy-start = (bf16[32,5120]{1,0:T(8,128)(2,1)S(1)}, bf16[32,5120]{1,0:T(8,128)(2,1)}, u32[]{:S(2)}) copy-start(bf16[32,5120]{1,0:T(8,128)(2,1)} %mlp.2) | copy-start | bytes 983044
Sparse Core Ops, SparseCore 0:
  11.2 29.6 all-gather.9
  45.7 41.6 all-gather.11
  89.6 41.5 all-gather.17
  148.2 33.0 reduce-scatter.2
  237.7 28.8 all-gather.13
  270.8 41.6 all-gather.15
  315.2 41.5 all-gather.19
  373.8 33.0 reduce-scatter.4

commit v2 on v0

v2 whole, which is shorter than its diff:
```python
import functools
import math
import jax
import jax.numpy as jnp
from jax import lax
from jax.experimental import pallas as pl
from jax.experimental.pallas import tpu as pltpu
from jax.sharding import PartitionSpec as P

HEAD_DIM = 128
HALF = HEAD_DIM // 2
ROPE_BASE = 1e4
NORM_EPS = 1e-5
SCORE_SCALE = HEAD_DIM ** -0.5
NX = 4
CORES = 2
NY = 4
NZ = 4
SEGMENTS = 4
COUNT_ROWS = 16
NCH = 10
PAIR = 2
AHEAD = 3
LAG_FAR = 3
LAG_USE = 2
RS_LAG_D = 2
RS_LAG_T = 6
RS_LAG_F = 12
WG_SLOTS = 2
WD_SLOTS = 4
VMEM_LIMIT = 63 * 1024 * 1024
BIG = 1e9
NEG = -1e30
MESH = pl.DeviceIdType.MESH
F32 = jnp.float32
BF16 = jnp.bfloat16
LEFT, RIGHT, FAR, P_OWN, P_LEFT, P_RIGHT, P_FAR, KINDS = range(8)
R_PAIR, R_FAR, R_NOW, R_PASS, R_KINDS = range(5)


def scope(name):
    return jax.named_scope(name)


def remote(ref, dst, send, recv, to):
    return pltpu.make_async_remote_copy(src_ref=ref, dst_ref=dst, send_sem=send, recv_sem=recv, device_id=to, device_id_type=MESH)


class Ring:
    def __init__(self):
        self.tp = lax.axis_index('tp')
        self.x = lax.div(self.tp, CORES)
        self.c = lax.rem(self.tp, CORES)
        self.right, self.left = self.dev(1), self.dev(-1)
        self.partner = {'tp': CORES * self.x + 1 - self.c}

    def at(self, dx):
        return lax.rem(self.x + dx + NX, NX)

    def dev(self, dx):
        return {'tp': CORES * self.at(dx) + self.c}


def sign(j):
    return 1 - 2 * lax.rem(j, 2)


def col(ref, j, width):
    return ref.at[:, pl.ds(pl.multiple_of(j * width, width), width)]


class Gather:
    def __init__(self, ring, buf, send, recv, rows, nch):
        self.g, self.buf, self.send, self.recv, self.rows, self.nch = ring, buf, send, recv, rows, nch

    def block(self, j, dx, core):
        r = pl.multiple_of((CORES * self.g.at(dx) + core) * self.rows, self.rows)
        return self.buf.at[j, pl.ds(r, self.rows), :]

    def copy(self, j, kind, dx, to):
        ref = self.block(j, dx, self.g.c)
        return remote(ref, ref, self.send.at[kind, j], self.recv.at[kind, j], to)

    def wait(self, j, kind):
        self.copy(j, kind, 0, self.g.partner).wait_recv()

    def start(self, j):
        self.copy(j, LEFT, 0, self.g.right).start()
        self.copy(j, RIGHT, 0, self.g.left).start()
        self.copy(j, P_OWN, 0, self.g.partner).start()

    def forward(self, j):
        self.wait(j, LEFT)
        self.wait(j, RIGHT)
        way = sign(j)
        self.copy(j, FAR, -way, self.g.dev(way)).start()
        self.copy(j, P_LEFT, -1, self.g.partner).start()
        self.copy(j, P_RIGHT, 1, self.g.partner).start()

    def forward_far(self, j):
        self.wait(j, FAR)
        self.copy(j, P_FAR, 2, self.g.partner).start()

    def drain(self):
        def body(j, _):
            for kind in range(KINDS):
                self.copy(j, kind, 0, self.g.partner).wait_send()
            return 0
        lax.fori_loop(0, self.nch, body, 0)

    def run(self, use, last):
        nch = self.nch
        for j in range(AHEAD):
            self.start(j)

        def whole(t):
            for i in range(PAIR):
                for kind in (P_OWN, P_LEFT, P_RIGHT, P_FAR):
                    self.wait(PAIR * t + i, kind)

        def body(t, _):
            for i in range(PAIR):
                s = PAIR * t + i

                @pl.when(s < nch)
                def _():
                    with scope('ag_fwd'):
                        self.forward(s)

                @pl.when(s + AHEAD < nch)
                def _():
                    self.start(s + AHEAD)

                @pl.when((s >= LAG_FAR) & (s - LAG_FAR < nch))
                def _():
                    with scope('ag_far'):
                        self.forward_far(s - LAG_FAR)

            @pl.when((t >= LAG_USE) & (t - LAG_USE < nch // PAIR - 1))
            def _():
                with scope('ag_whole'):
                    whole(t - LAG_USE)
                with scope('ag_use'):
                    use(t - LAG_USE)
            return 0
        lax.fori_loop(0, max(nch // PAIR - 1 + LAG_USE, pl.cdiv(nch + LAG_FAR, PAIR)), body, 0)
        with scope('ag_whole'):
            whole(nch // PAIR - 1)
        with scope('ag_last'):
            last()
        self.drain()


class Scatter:
    def __init__(self, ring, part, pair, passing, ends, own, out, send, recv, nch):
        self.g, self.part, self.pair, self.passing, self.ends, self.own, self.out = ring, part, pair, passing, ends, own, out
        self.send, self.recv, self.nch = send, recv, nch

    def copy(self, j, kind, src, dst, to):
        return remote(src, dst, self.send.at[kind, j], self.recv.at[kind, j], to)

    def pair_copy(self, j):
        return self.copy(j, R_PAIR, self.part.at[j, :, 1 - self.g.c], self.pair.at[j], self.g.partner)

    def near_copy(self, j, kind, way):
        side = lax.div(1 - way, 2)
        return self.copy(j, kind, self.out.at[j, side], self.ends.at[j, side], self.g.dev(way))

    def far_copy(self, j):
        return self.copy(j, R_FAR, self.out.at[j, 2], self.passing.at[j], self.g.dev(sign(j)))

    def stage_pair(self, j):
        self.pair_copy(j).wait_recv()
        g = self.g

        def both(dx):
            xx = g.at(dx)
            return self.part[j, xx, g.c].astype(F32) + self.pair[j, xx].astype(F32)
        self.out[j, 2] = both(2).astype(BF16)
        self.far_copy(j).start()
        self.out[j, 0] = both(1).astype(BF16)
        self.out[j, 1] = both(-1).astype(BF16)
        self.near_copy(j, R_NOW, -sign(j)).start()
        self.own[j] = both(0)

    def stage_pass(self, j):
        self.far_copy(j).wait_recv()
        side = lax.rem(j, 2)
        self.out[j, side] = (self.out[j, side].astype(F32) + self.passing[j].astype(F32)).astype(BF16)
        self.near_copy(j, R_PASS, sign(j)).start()

    def stage_end(self, j):
        for kind in (R_NOW, R_PASS):
            self.near_copy(j, kind, 1).wait_recv()
        return self.own[j] + self.ends[j, 0].astype(F32) + self.ends[j, 1].astype(F32)

    def drain(self):
        def body(j, _):
            self.pair_copy(j).wait_send()
            for kind in (R_FAR, R_NOW, R_PASS):
                self.near_copy(j, kind, 1).wait_send()
            return 0
        lax.fori_loop(0, self.nch, body, 0)

    def run(self, compute, finish):
        nch = self.nch

        def body(s, _):
            @pl.when(s < nch)
            def _():
                with scope('rs_compute'):
                    self.part[s] = compute(s)
                    self.pair_copy(s).start()

            @pl.when((s >= RS_LAG_D) & (s - RS_LAG_D < nch))
            def _():
                with scope('rs_pair'):
                    self.stage_pair(s - RS_LAG_D)

            @pl.when((s >= RS_LAG_T) & (s - RS_LAG_T < nch))
            def _():
                with scope('rs_pass'):
                    self.stage_pass(s - RS_LAG_T)

            @pl.when(s >= RS_LAG_F)
            def _():
                j = s - RS_LAG_F
                with scope('rs_end'):
                    finish(j, self.stage_end(j))
            return 0
        lax.fori_loop(0, nch + RS_LAG_F, body, 0)
        self.drain()


class Plane:
    def __init__(self):
        self.b = lax.axis_index('sp')
        self.z = lax.div(self.b, NY)
        self.y = lax.rem(self.b, NY)

    def index(self, first_y, df, ds):
        dy, dz = (df, ds) if first_y else (ds, df)
        return lax.rem(self.z + dz + NZ, NZ) * NY + lax.rem(self.y + dy + NY, NY)


class Spread:
    NEAR, STEPS = 3, 6
    FIRST = (0, -1, 1, 2)
    KINDS = NEAR + 3 * len(FIRST)

    def __init__(self, plane, first_y, view, send, recv):
        self.p, self.first_y, self.view, self.send, self.recv = plane, first_y, view, send, recv

    def copy(self, kind, df, ds, to_f, to_s):
        ref = self.view(self.p.index(self.first_y, df, ds))
        return remote(ref, ref, self.send(kind), self.recv(kind), {'sp': self.p.index(self.first_y, to_f, to_s)})

    def put(self, *a):
        self.copy(*a).start()

    def get(self, kind):
        self.copy(kind, 0, 0, 0, 1).wait_recv()

    def across(self, i):
        kind = self.NEAR + 3 * i
        self.put(kind, self.FIRST[i], 0, 0, 1)
        self.put(kind + 1, self.FIRST[i], 0, 0, -1)

    def far(self, i):
        kind = self.NEAR + 3 * i
        self.get(kind)
        self.get(kind + 1)
        way = 1 - 2 * (i % 2)
        self.put(kind + 2, self.FIRST[i], -way, 0, way)

    def step(self, n):
        if n == 0:
            self.put(0, 0, 0, 1, 0)
            self.put(1, 0, 0, -1, 0)
            self.across(0)
        elif n == 1:
            self.get(0)
            self.get(1)
            way = 1 if self.first_y else -1
            self.put(2, -way, 0, way, 0)
            self.across(1)
            self.across(2)
            self.far(0)
        elif n == 2:
            self.get(2)
            self.across(3)
        elif n == 3:
            self.far(1)
            self.far(2)
        elif n == 4:
            self.far(3)
        else:
            for i in range(len(self.FIRST)):
                self.get(self.NEAR + 3 * i + 2)

    def drain(self):
        for kind in range(self.KINDS):
            self.copy(kind, 0, 0, 0, 1).wait_send()


def enter(peers):
    barrier = pltpu.get_barrier_semaphore()
    for dev in peers:
        pl.semaphore_signal(barrier, inc=1, device_id=dev, device_id_type=MESH)
    pl.semaphore_wait(barrier, len(peers))


def joined(parts, axis=0):
    return parts[0] if len(parts) == 1 else jnp.concatenate(parts, axis=axis)


def stack_kernel(dims, x_hbm, aux_hbm, ga_ref, gm_ref, wq_hbm, wk_hbm, wv_hbm, wo_hbm, wg_hbm, wu_hbm, wd_hbm, out_ref, kc_ref, vc_ref,
                 x_ref, gains, aux, nbuf, wq, wkv, wo, qbuf, kbuf, vbuf, segq, sbuf, acc, m_ref, l_ref, obuf,
                 acc_g, acc_u, act, wgu, wd, part, pair, passing, ends, own, outs,
                 in_sem, wq_sem, wo_sem, gu_sem, wd_sem, c_sem, ag_send, ag_recv, ax_send, ax_recv, rs_send, rs_recv, kv_send, kv_recv):
    layers, rows, d_model, heads, units = dims
    cw = d_model // NCH
    chip = CORES * rows
    tokens = NX * chip
    g = Ring()
    p = Plane()
    me = pl.ds(pl.multiple_of(g.tp * rows, rows), rows)

    def attn_weights(layer):
        return [pltpu.make_async_copy(w.at[layer], to, wq_sem.at[i]) for i, (w, to) in enumerate(
            ((wk_hbm, wkv.at[:, pl.ds(0, HEAD_DIM)]), (wv_hbm, wkv.at[:, pl.ds(HEAD_DIM, HEAD_DIM)]), (wq_hbm, wq)))]

    def out_weights(layer):
        return [pltpu.make_async_copy(wo_hbm.at[layer, :, pl.ds(j * cw, cw)], wo.at[j], wo_sem.at[j]) for j in range(NCH)]

    def gu_copies(t):
        slot = lax.rem(t, WG_SLOTS)
        steps = NCH // PAIR
        r = pl.ds(pl.multiple_of(lax.rem(t, steps) * (PAIR * cw), PAIR * cw), PAIR * cw)
        return [pltpu.make_async_copy(w.at[lax.div(t, steps), r, :], wgu.at[slot, k], gu_sem.at[slot, k]) for k, w in enumerate((wg_hbm, wu_hbm))]

    def wd_copy(t):
        slot = lax.rem(t, WD_SLOTS)
        r = pl.ds(pl.multiple_of(lax.rem(t, NCH) * cw, cw), cw)
        return pltpu.make_async_copy(wd_hbm.at[lax.div(t, NCH), :, r], wd.at[slot], wd_sem.at[slot])

    def start_all(copies):
        for w in copies:
            w.start()

    def wait_all(copies):
        for w in copies:
            w.wait()

    first_in = [pltpu.make_async_copy(x_hbm, x_ref, in_sem.at[0]), pltpu.make_async_copy(aux_hbm, aux.at[0, me, :], in_sem.at[1])]
    start_all(first_in)
    start_all(attn_weights(0))
    start_all(out_weights(0))
    for t in range(WG_SLOTS):
        start_all(gu_copies(t))
    for t in range(WD_SLOTS):
        wd_copy(t).start()
    for i, ref in enumerate((ga_ref, gm_ref)):
        for layer in range(layers):
            gains[layer, i] = ref[layer:layer + 1, :].astype(F32)
    with scope('enter'):
        enter([g.right, g.left, g.partner] + [{'sp': p.index(True, df, ds)} for df, ds in ((1, 0), (-1, 0), (0, 1), (0, -1))])
        wait_all(first_in)

    ag = Gather(g, nbuf, ag_send, ag_recv, rows, NCH)
    ax = Gather(g, aux, ax_send, ax_recv, rows, 1)
    rs = Scatter(g, part, pair, passing, ends, own, outs, rs_send, rs_recv, NCH)
    half = lax.div(g.x, 2)
    par = lax.rem(g.x, 2)
    groups = ([(half, par)], [(0, 1 - par), (1, 1 - par)], [(1 - half, par)])
    NEXT = 1

    def norm(layer, which):
        with scope('norm'):
            x32 = x_ref[...].astype(F32)
            inv = lax.rsqrt(jnp.mean(x32 * x32, axis=-1, keepdims=True) + NORM_EPS)
            for j in range(NCH):
                sl = slice(j * cw, (j + 1) * cw)
                nbuf[j, me, :] = (x_ref[:, sl].astype(F32) * inv * gains[layer, which, :, sl]).astype(BF16)

    def finish(j, total):
        x_col = col(x_ref, j, cw)
        x_col[...] = (x_col[...].astype(F32) + total.astype(BF16).astype(F32)).astype(BF16)

    def chip_rows(ip):
        return pl.ds(pl.multiple_of((2 * ip[0] + ip[1]) * chip, chip), chip)

    def project(layer, grp):
        with scope('qkv%d' % grp):
            where = [chip_rows(ip) for ip in groups[grp]]
            q = k_v = None
            for j in range(NCH):
                lhs = joined([nbuf[j, r, :] for r in where])
                dq = jnp.dot(lhs, wq[j * cw:(j + 1) * cw, :], preferred_element_type=F32)
                dkv = jnp.dot(lhs, wkv[j * cw:(j + 1) * cw, :], preferred_element_type=F32)
                q = dq if q is None else q + dq
                k_v = dkv if k_v is None else k_v + dkv
            cosf = joined([aux[0, r, 0:HEAD_DIM] for r in where])
            sinf = joined([aux[0, r, HEAD_DIM:2 * HEAD_DIM] for r in where])

            def rope(v):
                return (v * cosf + pltpu.roll(v, HALF, 1) * sinf).astype(BF16)
            k_new = rope(k_v[:, :HEAD_DIM])
            v_new = k_v[:, HEAD_DIM:].astype(BF16)
            for i, (a, b) in enumerate(groups[grp]):
                sl = slice(i * chip, (i + 1) * chip)
                kbuf[layer, p.b, a, b, 0:chip] = k_new[sl]
                vbuf[layer, p.b, a, b] = v_new[sl]
                seg = aux[0, where[i], 2 * HEAD_DIM:3 * HEAD_DIM]
                counts = [jnp.sum(jnp.where(seg < float(v), 1.0, 0.0), axis=0, keepdims=True) for v in range(SEGMENTS)]
                kbuf[layer, p.b, a, b, chip:] = joined(counts + [jnp.zeros((COUNT_ROWS - SEGMENTS, HEAD_DIM), F32)]).astype(BF16)
            for h in range(heads):
                q_new = rope(q[:, h * HEAD_DIM:(h + 1) * HEAD_DIM])
                for i, r in enumerate(where):
                    qbuf[h, r, :] = q_new[i * chip:(i + 1) * chip]

    scale = SCORE_SCALE * math.log2(math.e)

    def scores(layer, zz, ip, slot):
        first = (2 * ip[0] + ip[1]) * chip
        keytok = lax.broadcasted_iota(jnp.int32, (chip, tokens), 0).astype(F32)
        qtok = (lax.broadcasted_iota(jnp.int32, (1, tokens), 1) - first).astype(F32)
        seg = segq[0:1, :]
        keys = kbuf[layer, pl.ds(zz * NY, NY), ip[0], ip[1], 0:chip].reshape(NY * chip, HEAD_DIM)
        raw = [lax.dot_general(keys, qbuf[h], (((1,), (1,)), ((), ())), preferred_element_type=F32) for h in range(heads)]
        for yy in range(NY):
            blk = zz * NY + yy
            cb = kbuf[layer, blk, ip[0], ip[1], chip:].astype(F32)
            low = jnp.zeros((1, tokens), F32)
            for v in range(1, SEGMENTS):
                n_v = joined([cb[v:v + 1]] * (tokens // HEAD_DIM), axis=1)
                low = low + jnp.where(seg == float(v), n_v, 0.0)
            rel = blk - p.b
            past = jnp.where(rel < 0, BIG, jnp.where(rel > 0, -BIG, 0.0))
            here = jnp.where(rel == 0, 1.0, 0.0)
            high = past + here * qtok
            bias = jnp.where((keytok >= low) & (keytok <= high), 0.0, NEG)
            sl = slice(yy * chip, (yy + 1) * chip)
            for h in range(heads):
                sbuf[slot, h, sl, :] = raw[h][sl] * scale + bias

    def absorb(layer, zz, ip, slot):
        vals_t = vbuf[layer, pl.ds(zz * NY, NY), ip[0], ip[1]].reshape(NY * chip, HEAD_DIM).T
        for h in range(heads):
            s = sbuf[slot, h]
            m_old = m_ref[h]
            m_new = jnp.maximum(m_old, jnp.max(s, axis=0, keepdims=True))
            alpha = jnp.exp2(m_old - m_new)
            w = jnp.exp2(s - m_new)
            l_ref[h] = l_ref[h] * alpha + jnp.sum(w, axis=0, keepdims=True)
            m_ref[h] = m_new
            acc[h] = acc[h] * alpha + jnp.dot(vals_t, w.astype(BF16), preferred_element_type=F32)

    def attend(layer, grp):
        chips = groups[grp]
        n = len(chips)
        total = (p.z + 1) * n

        def place(t):
            if n == 1:
                return t, chips[0]
            return lax.div(t, n), (lax.rem(t, n), chips[0][1])

        with scope('attend%d' % grp):
            scores(layer, *place(0), 0)

            def body(t, _):
                slot = lax.rem(t, 2)
                scores(layer, *place(lax.min(t + 1, total - 1)), 1 - slot)
                absorb(layer, *place(t), slot)
                return 0
            lax.fori_loop(0, total, body, 0)

    def attention_phase(layer):
        def view(buf, grp):
            if grp == NEXT:
                return lambda b: buf.at[layer, b, :, 1 - par]
            return lambda b: buf.at[layer, b, groups[grp][0][0], par]
        kv = [[Spread(p, buf is kbuf, view(buf, grp), (lambda kind, at=(grp, k): kv_send.at[layer, at[0], at[1], kind]),
                      (lambda kind, at=(grp, k): kv_recv.at[layer, at[0], at[1], kind]))
               for k, buf in enumerate((kbuf, vbuf))] for grp in range(len(groups))]

        def kv_step(grp, n):
            with scope('kv%d_%d' % (grp, n)):
                for s in kv[grp]:
                    s.step(n)

        def wait(*kinds):
            with scope('wait%d' % kinds[0]):
                for j in range(NCH):
                    for kind in kinds:
                        ag.wait(j, kind)

        def aux_wait(*kinds):
            @pl.when(layer == 0)
            def _():
                for kind in kinds:
                    ax.wait(0, kind)

        def fwd(lo, hi):
            with scope('fwd'):
                for j in range(lo, hi):
                    ag.forward(j)

        @pl.when(layer == 0)
        def _():
            ax.start(0)
        norm(layer, 0)
        early = AHEAD + 1
        for j in range(early):
            ag.start(j)
        aux_wait(P_OWN)
        for j in range(early, NCH):
            ag.copy(j, P_OWN, 0, g.partner).start()
        wait(P_OWN)
        wait_all(attn_weights(layer))
        project(layer, 0)
        kv_step(0, 0)

        @pl.when(layer == 0)
        def _():
            ax.forward(0)
        for j in range(early, NCH):
            ag.copy(j, LEFT, 0, g.right).start()
            ag.copy(j, RIGHT, 0, g.left).start()
        fwd(0, early)
        kv_step(0, 1)
        fwd(early, NCH - AHEAD)

        @pl.when(layer == 0)
        def _():
            ax.forward_far(0)
        kv_step(0, 2)
        kv_step(0, 3)
        fwd(NCH - AHEAD, NCH)
        wait(P_LEFT, P_RIGHT)
        aux_wait(P_LEFT, P_RIGHT)
        project(layer, NEXT)
        kv_step(NEXT, 0)
        kv_step(0, 4)
        with scope('fwd_far'):
            for j in range(NCH):
                ag.forward_far(j)
        kv_step(NEXT, 1)
        wait(P_FAR)

        @pl.when(layer == 0)
        def _():
            ax.wait(0, P_FAR)
            segq[...] = aux[0, :, 2 * HEAD_DIM:3 * HEAD_DIM].T[0:segq.shape[0], :]
        project(layer, 2)
        kv_step(2, 0)

        @pl.when(layer + 1 < layers)
        def _():
            start_all(attn_weights(layer + 1))
        kv_step(NEXT, 2)
        kv_step(0, 5)
        acc[...] = jnp.zeros_like(acc)
        l_ref[...] = jnp.zeros_like(l_ref)
        m_ref[...] = jnp.full_like(m_ref, NEG)
        attend(layer, 0)
        kv_step(NEXT, 3)
        kv_step(2, 1)
        kv_step(NEXT, 4)
        kv_step(2, 2)
        kv_step(2, 3)
        kv_step(NEXT, 5)
        attend(layer, NEXT)
        kv_step(2, 4)
        kv_step(2, 5)
        attend(layer, 2)
        with scope('heads'):
            for h in range(heads):
                obuf[:, h * HEAD_DIM:(h + 1) * HEAD_DIM] = (acc[h] / l_ref[h]).T.astype(BF16)
            caches = [pltpu.make_async_copy(kbuf.at[layer, p.b, :, :, pl.ds(0, chip)], kc_ref.at[layer], c_sem.at[0]),
                      pltpu.make_async_copy(vbuf.at[layer, p.b], vc_ref.at[layer], c_sem.at[1])]
            start_all(caches)
            ag.drain()
            wait_all(out_weights(layer))

        def proj_out(j):
            return jnp.dot(obuf[...], wo[j], preferred_element_type=F32).astype(BF16).reshape(NX, CORES, rows, cw)
        rs.run(proj_out, finish)
        with scope('drain'):
            @pl.when(layer + 1 < layers)
            def _():
                start_all(out_weights(layer + 1))

            @pl.when(layer == 0)
            def _():
                ax.drain()
            for grp in kv:
                for s in grp:
                    s.drain()
            wait_all(caches)

    def mlp_phase(layer):
        steps = NCH // PAIR
        norm(layer, 1)
        acc_g[...] = jnp.zeros_like(acc_g)
        acc_u[...] = jnp.zeros_like(acc_u)

        def lhs(t, i):
            return nbuf[PAIR * t + i]

        def refill(t):
            @pl.when(t + WG_SLOTS < layers * steps)
            def _():
                start_all(gu_copies(t + WG_SLOTS))

        def half_dot(t, k, slot, sl):
            return sum(jnp.dot(lhs(t, i), wgu[slot, k, i * cw:(i + 1) * cw, sl], preferred_element_type=F32) for i in range(PAIR))

        def gate_up(t):
            at = layer * steps + t
            wait_all(gu_copies(at))
            slot = lax.rem(at, WG_SLOTS)
            for k, into in enumerate((acc_g, acc_u)):
                into[...] += half_dot(t, k, slot, slice(None))
            refill(at)

        def gate_up_last():
            t = steps - 1
            at = layer * steps + t
            wait_all(gu_copies(at))
            slot = lax.rem(at, WG_SLOTS)
            step = min(CORES * HEAD_DIM, units)
            for lo in range(0, units, step):
                sl = slice(lo, lo + step)
                gate = acc_g[:, sl] + half_dot(t, 0, slot, sl)
                up = acc_u[:, sl] + half_dot(t, 1, slot, sl)
                act[:, sl] = (gate * jax.nn.sigmoid(gate) * up).astype(BF16)
            refill(at)

        ag.run(gate_up, gate_up_last)

        def down(j):
            at = layer * NCH + j
            wd_copy(at).wait()
            res = jnp.dot(act[...], wd[lax.rem(at, WD_SLOTS)], preferred_element_type=F32).astype(BF16)

            @pl.when(at + WD_SLOTS < layers * NCH)
            def _():
                wd_copy(at + WD_SLOTS).start()
            return res.reshape(NX, CORES, rows, cw)
        rs.run(down, finish)

    def layer_body(layer, _):
        attention_phase(layer)
        mlp_phase(layer)
        return 0
    lax.fori_loop(0, layers, layer_body, 0)
    out_ref[...] = x_ref[...]


def stack_call(hidden, aux, attn_gain, mlp_gain, w_q, w_k, w_v, w_o, w_gate, w_up, w_down):
    rows, d_model = hidden.shape
    layers = w_q.shape[0]
    cw = d_model // NCH
    q_dim, units = w_q.shape[2], w_gate.shape[2]
    heads = q_dim // HEAD_DIM
    chip = CORES * rows
    tokens = NX * chip
    blocks = NY * NZ
    hbm = pl.BlockSpec(memory_space=pl.ANY)
    vmem = pl.BlockSpec(memory_space=pltpu.VMEM)
    dma = pltpu.SemaphoreType.DMA
    cache = jax.ShapeDtypeStruct((layers, 2, 2, chip, HEAD_DIM), BF16)

    def b16(*shape):
        return pltpu.VMEM(shape, BF16)

    def f32(*shape):
        return pltpu.VMEM(shape, F32)
    out, k_c, v_c = pl.pallas_call(
        functools.partial(stack_kernel, (layers, rows, d_model, heads, units)),
        out_shape=(jax.ShapeDtypeStruct((rows, d_model), BF16), cache, cache),
        in_specs=[hbm, hbm, vmem, vmem] + [hbm] * 7,
        out_specs=(vmem, hbm, hbm),
        scratch_shapes=[
            b16(rows, d_model), f32(layers, 2, 1, d_model), f32(1, tokens, 3 * HEAD_DIM), b16(NCH, tokens, cw),
            b16(d_model, q_dim), b16(d_model, 2 * HEAD_DIM), b16(NCH, q_dim, cw), b16(heads, tokens, HEAD_DIM),
            b16(layers, blocks, 2, 2, chip + COUNT_ROWS, HEAD_DIM), b16(layers, blocks, 2, 2, chip, HEAD_DIM),
            f32(8, tokens), f32(2, heads, NY * chip, tokens), f32(heads, HEAD_DIM, tokens), f32(heads, 1, tokens), f32(heads, 1, tokens),
            b16(tokens, q_dim),
            f32(tokens, units), f32(tokens, units), b16(tokens, units), b16(WG_SLOTS, 2, PAIR * cw, units), b16(WD_SLOTS, units, cw),
            b16(NCH, NX, CORES, rows, cw), b16(NCH, NX, rows, cw), b16(NCH, rows, cw), b16(NCH, 2, rows, cw), f32(NCH, rows, cw),
            b16(NCH, 3, rows, cw),
            dma((2,)), dma((3,)), dma((NCH,)), dma((WG_SLOTS, 2)), dma((WD_SLOTS,)), dma((2,)),
            dma((KINDS, NCH)), dma((KINDS, NCH)), dma((KINDS, 1)), dma((KINDS, 1)), dma((R_KINDS, NCH)), dma((R_KINDS, NCH)),
            dma((layers, 3, 2, Spread.KINDS)), dma((layers, 3, 2, Spread.KINDS)),
        ],
        compiler_params=pltpu.CompilerParams(collective_id=0, has_side_effects=True, vmem_limit_bytes=VMEM_LIMIT),
        name='stack',
    )(hidden, aux, attn_gain, mlp_gain, w_q, w_k, w_v, w_o, w_gate, w_up, w_down)
    return out, k_c.reshape(layers, tokens, 1, HEAD_DIM), v_c.reshape(layers, tokens, 1, HEAD_DIM)


def aux_table(positions, segment_ids):
    inv_freq = ROPE_BASE ** (-jnp.arange(HALF, dtype=jnp.float32) / HALF)
    angles = positions.astype(jnp.float32)[:, None] * inv_freq
    cos_val = jnp.cos(angles)
    sin_val = jnp.sin(angles)
    seg = jnp.broadcast_to(segment_ids.astype(F32)[:, None], (positions.shape[0], HEAD_DIM))
    return jnp.concatenate([cos_val, cos_val, -sin_val, sin_val, seg], axis=-1)


def solution(mesh):
    tok_spec = P(('dp', 'sp', 'tp'))
    row_block = P(('dp', 'sp', 'tp'), None)
    col_spec = P(None, None, 'tp')
    row_spec = P(None, 'tp', None)
    cache_spec = P(None, ('dp', 'sp'), 'tp', None)

    def device_fn(hidden_in, segment_ids, positions, attn_gain, w_q, w_k, w_v, w_o, mlp_gain, w_gate, w_up, w_down):
        aux = aux_table(positions, segment_ids)
        return stack_call(hidden_in, aux, attn_gain, mlp_gain, w_q, w_k, w_v, w_o, w_gate, w_up, w_down)

    return jax.shard_map(device_fn, mesh=mesh,
                         in_specs=(row_block, tok_spec, tok_spec, P(), col_spec, col_spec, col_spec, row_spec, P(), col_spec, col_spec, row_spec),
                         out_specs=(row_block, cache_spec, cache_spec), check_vma=False)
```

time: 554 us -> 231 us (0.42)
  the two profiles are of different devices: /device:TPU:1 before, /device:TPU:68 now
where the time goes in v2:
time: 231 us; the launch traced here: 230 us
  Pallas kernels  223 us (97%)
  local copies, waits for them, and re-layouts  5.62 us (2%)
    pallas_call x1, Pallas kernels, stack_call(): pl.pallas_call(functools.partial(stack_kernel, (layers, rows, d_model, he...  223 us
    unnamed x3, local copies, waits for them, and re-layouts  4.85 us

profile of v2, /device:TPU:68, one launch (start us, length us, event | category | flops | bytes accessed | tf_op | source)
XLA Modules:
  0.0 230.3 jit_solution(18019398488530926388)
XLA Ops:
  0.6 0.7 convert_element_type.7
  1.3 0.7 convert_element_type.6
  2.0 0.1 broadcast_in_dim.2
  2.0 0.1 multiply_sine_fusion
  2.2 0.7 concatenate.3.aux_hbm
  2.9 222.6 %stack.1 = (bf16[32,5120]{1,0:T(8,128)(2,1)}, bf16[2,2,2,64,128]{4,3,2,1,0:T(8,128)(2,1)}, bf16[2,2,2,64,128]{4,3,2,1,0:T(8,128)(2,1)}) custom-call(bf16[32,5120]{1,0:T(8,128)(2,1)} %x_hbm.1, f32[32,384]{1,0:T(8,128)} %concatenate.3.aux_hbm, bf16[2,5120]{1,0:T(2,128)(2,1)} %ga_ref.1, bf16[2,5120]{1,0:T(2,128)(2,1)} %gm_ref.1, bf16[2,5120,512]{2,1,0:T(8,128)(2,1)} %wq_hbm.1, ...), custom_call_target="tpu_custom_call" | custom-call | tf_op jit(solution)/shard_map/stack/pallas_call | solution.py:681
  225.5 1.7 copy.20
  227.2 1.6 copy.21
  228.7 1.6 copy.22
  (1 shorter events, 0.0 us)
